TPU v7x, 32 devices: a whole 2x2x4 slice. The times are simulated.
32 devices in a mesh: lat: 8 (over z, core), wave: 4 (over y, x).
Axes of the slice: x: 2, y: 2, z: 4, core: 2. Of those that a mesh axis runs over, the one named last changes fastest.
Arguments:
- spectra: bfloat16 [3, 2, 2, 768, 768], P(None, None, None, 'wave', 'lat'), may hold values from -0.01171875 to 0.01171875
- legendre: bfloat16 [16, 768, 768], P('lat', 'wave'), may hold values from -4 to 4
- wave_m: int32 [768], replicated, may hold values from 0 to 767, each once
- nlon: int32 [16], P('lat'), may hold values from 20 to 3088, as said below
- coriolis: float32 [16], P('lat'), may hold values from -1.5 to 1.5
- gauss_quadrature_weight: float32 [16], P('lat'), may hold values from 0.5 to 5
Outputs:
- tendency: float32 [2, 2, 2, 768, 768], P(None, None, None, 'wave', 'lat')
Inputs may be any that keep to these rules, and one draw needn't show every extreme that they name: `nlon`: each value is 20 + 4 i for a whole number i, and some latitude has 3088. `wave_m`: every wavenumber 0 to 767 stands in exactly one slot.
All inputs are finite; a program needn't handle non-finite values.
Results may differ from a plain program's by a relative error of at most 0.0065.
Values may be sent and summed in bfloat16 or wider, within the bound.
No kernel may reach another device: no remote copies, remote signals or barrier semaphores. Data moves between devices by JAX's collectives and lax.ppermute only.
A program may use at most 64 MiB of HBM per device.

v0:
```python
import jax
import jax.numpy as jnp
from jax import lax
from jax.sharding import PartitionSpec as P

NLON = 3088
lon_block = 512
two_pi = 6.283185307179586


def block_count():
    return (NLON + lon_block - 1) // lon_block


def pick_entry(values, position):
    positions = jnp.arange(values.shape[0], dtype=jnp.int32)
    return jnp.sum(jnp.where(positions == position, values, jnp.zeros_like(values)))


def column_factor(wave_ids, count):
    doubled = jnp.where(wave_ids == 0, jnp.float32(1.0), jnp.float32(2.0))
    return jnp.where(2 * wave_ids < count, doubled, jnp.float32(0.0))


def phase_table(wave_ids, first_place, count):
    places = first_place + jnp.arange(lon_block, dtype=jnp.int32)
    residue = places[:, None] * wave_ids[None, :] % count
    angles = two_pi * residue.astype(jnp.float32) / count.astype(jnp.float32)
    return jnp.concatenate([jnp.cos(angles), jnp.sin(angles)], axis=1).astype(jnp.bfloat16)


def inverse_stack(coefficient, multiplier):
    real_part = coefficient[..., 0, :].astype(jnp.float32) * multiplier
    imag_part = -coefficient[..., 1, :].astype(jnp.float32) * multiplier
    return jnp.concatenate([real_part, imag_part], axis=-1).astype(jnp.bfloat16)


def nonlinear(nodal_samples, rotation, places, count):
    vorticity = nodal_samples[..., 0, :]
    velocity_spread_map = nodal_samples[..., 1, :]
    thermal_state_map = nodal_samples[..., 2, :]
    stretch = -(vorticity + rotation) * velocity_spread_map
    thermal_forcing = -thermal_state_map * velocity_spread_map
    paired = jnp.stack([stretch, thermal_forcing], axis=-2)
    return jnp.where(places < count, paired, jnp.zeros_like(paired)).astype(jnp.bfloat16)


def finish(summed_spectra, multiplier, count, weight):
    halfway = summed_spectra.shape[-1] // 2
    scaling_factor = weight / count.astype(jnp.float32)
    real_part = summed_spectra[..., :halfway] * scaling_factor
    imag_part = -summed_spectra[..., halfway:] * scaling_factor
    paired = jnp.stack([real_part, imag_part], axis=-2)
    return jnp.where(multiplier > 0, paired, jnp.zeros_like(paired)).astype(jnp.bfloat16)


def grid_row(piled_arrays, wave_ids, count, rotation, weight, multiplier):

    def one_block(running, block_index):
        first_place = block_index * lon_block
        phases = phase_table(wave_ids, first_place, count)
        nodal_samples = lax.dot_general(
            piled_arrays, phases, (((1,), (1,)), ((), ())), preferred_element_type=jnp.float32
        )
        nodal_samples = nodal_samples.reshape(-1, 3, lon_block)
        places = first_place + jnp.arange(lon_block, dtype=jnp.int32)
        products = nonlinear(nodal_samples, rotation, places, count).reshape(-1, lon_block)
        return (running + jnp.dot(products, phases, preferred_element_type=jnp.float32), None)

    zero_sums = jnp.zeros((piled_arrays.shape[0] // 3 * 2, piled_arrays.shape[1]), jnp.float32)
    summed_spectra, unused = lax.scan(
        one_block, zero_sums, jnp.arange(block_count(), dtype=jnp.int32)
    )
    return finish(summed_spectra.reshape(-1, 2, piled_arrays.shape[1]), multiplier, count, weight)


def local(spectra, legendre, wave_m, nlon, coriolis, gauss_quadrature_weight):
    band_lats, slot_count, wave_total = legendre.shape
    lev_count = spectra.shape[1]
    band_rows = band_lats * lev_count
    wave_rank = lax.axis_index("wave")
    local_ids = lax.dynamic_slice_in_dim(wave_m, wave_rank * slot_count, slot_count, 0)
    totals = jnp.arange(wave_total, dtype=jnp.int32)
    masked = jnp.where(
        totals[None, None, :] >= local_ids[None, :, None], legendre, jnp.zeros_like(legendre)
    )

    def row_facts(row_number):
        latitude_row = row_number // lev_count
        return (
            pick_entry(nlon, latitude_row),
            pick_entry(coriolis, latitude_row),
            pick_entry(gauss_quadrature_weight, latitude_row),
        )

    band_part = masked
    fourier = jnp.einsum(
        "lsn,fvpsn->lvfps",
        band_part,
        lax.all_gather(spectra, "lat", axis=4, tiled=True),
        preferred_element_type=jnp.float32,
    ).astype(jnp.bfloat16)
    fourier = fourier.reshape(band_rows, 3, 2, slot_count)
    gathered = lax.all_to_all(fourier, "wave", split_axis=0, concat_axis=3, tiled=True)
    owned_latitude_rows = gathered.shape[0]

    def full_row(inputs):
        coefficient, offset = inputs
        count, rotation, weight = row_facts(wave_rank * owned_latitude_rows + offset)
        multiplier = column_factor(wave_m, count)
        piled_arrays = inverse_stack(coefficient, multiplier)
        return grid_row(piled_arrays, wave_m, count, rotation, weight, multiplier)[0]

    local_rows = lax.map(full_row, (gathered, jnp.arange(owned_latitude_rows, dtype=jnp.int32)))
    returned = lax.all_to_all(local_rows, "wave", split_axis=3, concat_axis=0, tiled=True)
    returned = returned.reshape(band_lats, lev_count, 2, 2, slot_count)
    turned = lax.all_to_all(masked, "lat", split_axis=2, concat_axis=0, tiled=True)
    band_part = turned
    return jnp.einsum(
        "lsn,lvqps->qvpsn",
        band_part,
        lax.all_gather(returned, "lat", axis=0, tiled=True),
        preferred_element_type=jnp.float32,
    )


def solution(mesh):
    placed = (
        P(None, None, None, "wave", "lat"),
        P("lat", "wave", None),
        P(),
        P("lat"),
        P("lat"),
        P("lat"),
    )
    return jax.shard_map(
        local,
        mesh=mesh,
        in_specs=placed,
        out_specs=P(None, None, None, "wave", "lat"),
        check_vma=False,
    )
```

profile of v0, /device:TPU:0, one launch (start us, length us, event | category | flops | bytes accessed | tf_op | source)
XLA Modules:
  0.0 325.8 jit_solution(5381453114664748880)
XLA Ops:
  6.5 2.2 copy.49
  8.7 0.6 copy.48
  9.6 1.3 fusion.32
  11.0 1.5 copy.61
  12.5 0.6 select_reduce_fusion.2
  13.1 0.6 broadcast_compare_fusion.1
  13.8 2.2 broadcast_select_fusion
  16.0 47.0 %all-gather.2.cloned.1.call-done = bf16[3,2,2,192,768]{3,2,1,0,4:T(2,128)(2,1)} async-done(((bf16[3,2,2,192,96]{3,2,1,0,4:T(2,128)(2,1)}), bf16[3,2,2,192,768]{3,2,1,0,4:T(2,128)(2,1)}) %all-gather.2.cloned.1.call-update) | async-done | bytes 3538960 | tf_op jit(solution)/shard_map/all_gather | solution.py:100
  62.9 16.6 %copy.51 = bf16[3,2,2,192,768]{4,0,2,1,3:T(4,128)(2,1)} copy(bf16[3,2,2,192,768]{3,2,1,0,4:T(2,128)(2,1)} %all-gather.2.cloned.1.call-done) | data formatting | bytes 7077888 | tf_op jit(solution)/shard_map/all_gather | solution.py:100
  79.6 23.1 %fusion.19 = bf16[2,2,3,2,192]{2,0,3,1,4:T(2,128)(2,1)S(1)} fusion(bf16[2,192,768,1,1]{2,0,4,3,1:T(2,128)(2,1)S(1)} %copy.61, bf16[3,2,2,192,768]{4,0,2,1,3:T(4,128)(2,1)} %copy.51), kind=kOutput, calls=%fused_computation.33 | convolution fusion | flops 7082496 | bytes 4137984 | tf_op jit(solution)/shard_map/lsn,fvpsn->lvfps/dot_general | solution.py:97
  102.7 1.1 copy.52
  103.8 3.6 %all-to-all-start = ((bf16[4,3,2,192]{3,2,1,0:T(2,128)(2,1)}), bf16[4,3,2,192]{3,2,1,0:T(2,128)(2,1)S(1)}, u32[]{:S(2)}, u32[]{:S(2)}) async-start(bf16[4,3,2,192]{3,2,1,0:T(2,128)(2,1)} %bitcast.2), calls=%async_computation | async-start | bytes 24576 | tf_op jit(solution)/shard_map/all_to_all | solution.py:104
  107.4 0.7 select_reduce_fusion
  110.7 1.5 all-to-all-done
  112.1 3.5 %all-to-all-start.2 = ((bf16[2,192,768]{1,0,2:T(2,128)(2,1)}), bf16[2,192,768]{1,0,2:T(2,128)(2,1)S(1)}, u32[]{:S(2)}, u32[]{:S(2)}) async-start(bf16[2,192,768]{1,0,2:T(2,128)(2,1)} %broadcast_select_fusion), calls=%async_computation.2 | async-start | bytes 1572864 | tf_op jit(solution)/shard_map/all_to_all | solution.py:117
  115.8 175.8 %while.20 = (s32[]{:T(128)}, f32[2,1536]{1,0:T(2,128)S(1)}, s32[7]{0:T(128)S(1)}, s32[]{:T(128)}, s32[768]{0:T(1024)S(1)}, /*index=5*/s32[]{:T(128)}, pred[]{:T(...) while((s32[]{:T(128)}, f32[2,1536]{1,0:T(2,128)S(1)}, ...), condition=%wide.region_3.4_spmd.clone, body=%wide.region_2.3_spmd.clone.sunk | while | flops 19283972 | bytes 4777152 | solution.py:71
  115.9 0.6 dynamic_slice.18
  117.1 0.6 broadcast_compare_fusion.3
  117.8 21.8 %cosine_convert_fusion.2 = (bf16[512,768]{1,0:T(8,128)(2,1)S(1)}, bf16[512,768]{1,0:T(8,128)(2,1)S(1)}) fusion(f32[]{:T(128)} %get-tuple-element.295, pred[]{:T(512)} %get-tuple-element.294, s32[]{:T(128)} %get-tuple-element.293, s32[768]{0:T(1024)S(1)} %get-tuple-element.292, s32[512]{0:T(512)S(1)} %iota_add_fusion.2), kind=kLoop, calls=%fused_computation.7.clone.1 | loop fusion | flops 5111808 | bytes 1577993 | tf_op jit(solution)/shard_map/convert
  139.6 0.5 convolution_bitcast_fusion.3
  140.1 0.6 fusion.38
  140.7 0.3 convolution_add_fusion.2
  141.0 0.6 dynamic_slice.18
  142.2 0.6 broadcast_compare_fusion.3
  142.9 21.8 %cosine_convert_fusion.2 = (bf16[512,768]{1,0:T(8,128)(2,1)S(1)}, bf16[512,768]{1,0:T(8,128)(2,1)S(1)}) fusion(f32[]{:T(128)} %get-tuple-element.295, pred[]{:T(512)} %get-tuple-element.294, s32[]{:T(128)} %get-tuple-element.293, s32[768]{0:T(1024)S(1)} %get-tuple-element.292, s32[512]{0:T(512)S(1)} %iota_add_fusion.2), kind=kLoop, calls=%fused_computation.7.clone.1 | loop fusion | flops 5111808 | bytes 1577993 | tf_op jit(solution)/shard_map/convert
  164.7 0.5 convolution_bitcast_fusion.3
  165.2 0.6 fusion.38
  165.8 0.3 convolution_add_fusion.2
  166.1 0.6 dynamic_slice.18
  167.3 0.6 broadcast_compare_fusion.3
  168.0 21.8 %cosine_convert_fusion.2 = (bf16[512,768]{1,0:T(8,128)(2,1)S(1)}, bf16[512,768]{1,0:T(8,128)(2,1)S(1)}) fusion(f32[]{:T(128)} %get-tuple-element.295, pred[]{:T(512)} %get-tuple-element.294, s32[]{:T(128)} %get-tuple-element.293, s32[768]{0:T(1024)S(1)} %get-tuple-element.292, s32[512]{0:T(512)S(1)} %iota_add_fusion.2), kind=kLoop, calls=%fused_computation.7.clone.1 | loop fusion | flops 5111808 | bytes 1577993 | tf_op jit(solution)/shard_map/convert
  189.8 0.5 convolution_bitcast_fusion.3
  190.3 0.6 fusion.38
  191.2 0.6 dynamic_slice.18
  192.5 0.6 broadcast_compare_fusion.3
  193.1 21.8 %cosine_convert_fusion.2 = (bf16[512,768]{1,0:T(8,128)(2,1)S(1)}, bf16[512,768]{1,0:T(8,128)(2,1)S(1)}) fusion(f32[]{:T(128)} %get-tuple-element.295, pred[]{:T(512)} %get-tuple-element.294, s32[]{:T(128)} %get-tuple-element.293, s32[768]{0:T(1024)S(1)} %get-tuple-element.292, s32[512]{0:T(512)S(1)} %iota_add_fusion.2), kind=kLoop, calls=%fused_computation.7.clone.1 | loop fusion | flops 5111808 | bytes 1577993 | tf_op jit(solution)/shard_map/convert
  214.9 0.5 convolution_bitcast_fusion.3
  215.4 0.6 fusion.38
  216.3 0.6 dynamic_slice.18
  217.6 0.6 broadcast_compare_fusion.3
  218.2 21.8 %cosine_convert_fusion.2 = (bf16[512,768]{1,0:T(8,128)(2,1)S(1)}, bf16[512,768]{1,0:T(8,128)(2,1)S(1)}) fusion(f32[]{:T(128)} %get-tuple-element.295, pred[]{:T(512)} %get-tuple-element.294, s32[]{:T(128)} %get-tuple-element.293, s32[768]{0:T(1024)S(1)} %get-tuple-element.292, s32[512]{0:T(512)S(1)} %iota_add_fusion.2), kind=kLoop, calls=%fused_computation.7.clone.1 | loop fusion | flops 5111808 | bytes 1577993 | tf_op jit(solution)/shard_map/convert
  240.0 0.5 convolution_bitcast_fusion.3
  240.5 0.6 fusion.38
  241.4 0.6 dynamic_slice.18
  242.7 0.6 broadcast_compare_fusion.3
  243.3 21.8 %cosine_convert_fusion.2 = (bf16[512,768]{1,0:T(8,128)(2,1)S(1)}, bf16[512,768]{1,0:T(8,128)(2,1)S(1)}) fusion(f32[]{:T(128)} %get-tuple-element.295, pred[]{:T(512)} %get-tuple-element.294, s32[]{:T(128)} %get-tuple-element.293, s32[768]{0:T(1024)S(1)} %get-tuple-element.292, s32[512]{0:T(512)S(1)} %iota_add_fusion.2), kind=kLoop, calls=%fused_computation.7.clone.1 | loop fusion | flops 5111808 | bytes 1577993 | tf_op jit(solution)/shard_map/convert
  265.1 0.5 convolution_bitcast_fusion.3
  265.6 0.6 fusion.38
  266.6 0.6 dynamic_slice.18
  267.8 0.6 broadcast_compare_fusion.3
  268.5 21.8 %cosine_convert_fusion.2 = (bf16[512,768]{1,0:T(8,128)(2,1)S(1)}, bf16[512,768]{1,0:T(8,128)(2,1)S(1)}) fusion(f32[]{:T(128)} %get-tuple-element.295, pred[]{:T(512)} %get-tuple-element.294, s32[]{:T(128)} %get-tuple-element.293, s32[768]{0:T(1024)S(1)} %get-tuple-element.292, s32[512]{0:T(512)S(1)} %iota_add_fusion.2), kind=kLoop, calls=%fused_computation.7.clone.1 | loop fusion | flops 5111808 | bytes 1577993 | tf_op jit(solution)/shard_map/convert
  290.2 0.5 convolution_bitcast_fusion.3
  290.8 0.6 fusion.38
  291.7 0.4 copy.56
  292.2 1.1 reshape.136
  293.3 3.2 all-to-all-start.1
  296.5 1.0 copy.58
  297.5 3.7 %all-to-all-done.1 = bf16[4,2,384]{2,1,0:T(2,128)(2,1)S(1)} async-done(((bf16[4,2,384]{2,1,0:T(2,128)(2,1)}), bf16[4,2,384]{2,1,0:T(2,128)(2,1)S(1)}, u32[]{:S(2)}, u32[]{:S(2)}) %all-to-all-start.1) | async-done | bytes 6176 | tf_op jit(solution)/shard_map/all_to_all | solution.py:115
  301.1 0.8 reshape.137
  302.0 0.3 copy.57
  302.3 14.4 %all_gather.7 = bf16[16,2,2,2,192]{4,3,2,1,0:T(2,128)(2,1)S(1)} all-gather(bf16[2,2,2,2,192]{4,3,2,1,0:T(2,128)(2,1)S(1)} %bitcast.68), channel_id=1, replica_groups=mesh['lat'=8,'wave'=4] {'lat'}, dimensions={0}, use_global_device_ids=true | all-gather | bytes 55296 | tf_op jit(solution)/shard_map/all_gather | solution.py:122
  316.7 0.4 copy.59
  317.2 0.7 convolution_bitcast_fusion.1
  317.9 1.0 copy.60
  (37 shorter events, 2.1 us)
Async XLA Ops:
  6.5 2.2 copy-start
  6.5 2.9 copy-start.1
  6.5 56.4 %all-gather.2.cloned.1.call-start = ((), (), s32[]{:S(2)}) async-start(), calls=%async_computation.3 | async-start | bytes 5308416 | tf_op jit(solution)/shard_map/all_gather | solution.py:100
  9.6 2.9 copy-start.4
  79.6 27.8 %copy-start.2 = (f32[2]{0:T(128)S(1)}, f32[2]{0:T(128)}, u32[]{:S(2)}) copy-start(f32[2]{0:T(128)} %param.13) | copy-start | bytes 28
  79.6 27.8 %copy-start.3 = (f32[2]{0:T(128)S(1)}, f32[2]{0:T(128)}, u32[]{:S(2)}) copy-start(f32[2]{0:T(128)} %param.12) | copy-start | bytes 28
  103.8 8.3 %all-to-all-start = ((bf16[4,3,2,192]{3,2,1,0:T(2,128)(2,1)}), bf16[4,3,2,192]{3,2,1,0:T(2,128)(2,1)S(1)}, u32[]{:S(2)}, u32[]{:S(2)}) async-start(bf16[4,3,2,192]{3,2,1,0:T(2,128)(2,1)} %bitcast.2), calls=%async_computation | async-start | bytes 24576 | tf_op jit(solution)/shard_map/all_to_all | solution.py:104
  112.1 181.1 %all-to-all-start.2 = ((bf16[2,192,768]{1,0,2:T(2,128)(2,1)}), bf16[2,192,768]{1,0,2:T(2,128)(2,1)S(1)}, u32[]{:S(2)}, u32[]{:S(2)}) async-start(bf16[2,192,768]{1,0,2:T(2,128)(2,1)} %broadcast_select_fusion), calls=%async_computation.2 | async-start | bytes 1572864 | tf_op jit(solution)/shard_map/all_to_all | solution.py:117
  293.3 7.9 %all-to-all-start.1 = ((bf16[4,2,384]{2,1,0:T(2,128)(2,1)}), bf16[4,2,384]{2,1,0:T(2,128)(2,1)S(1)}, u32[]{:S(2)}, u32[]{:S(2)}) async-start(bf16[4,2,384]{2,1,0:T(2,128)(2,1)} %reshape.136), calls=%async_computation.1 | async-start | bytes 12288 | tf_op jit(solution)/shard_map/all_to_all | solution.py:115
Sparse Core Ops, SparseCore 0:
  9.0 53.9 all-gather.1
where the time goes:
time: 327 us; the launch traced here: 326 us
  other arithmetic  167 us (51%)
  waiting for transfers between devices  52.1 us (16%)
  local copies, waits for them, and re-layouts  31.6 us (10%)
  matrix products  29.6 us (9%)
  between operations  16.2 us (5%)
  blocking collectives  14.4 us (4%)
  starting transfers between devices  10.4 us (3%)
  loops' own time  4.72 us (1%)
    another operation x8, other arithmetic  153 us
    all_gather x1, waiting for transfers between devices, local(): lax.all_gather(spectra, 'lat', axis=4, tiled=True)  47 us
    dot_general x1, matrix products, local(): jnp.einsum('lsn,fvpsn->lvfps', band_part, lax.all_gather(spectra, 'lat',...  23.1 us
    all_gather x1, local copies, waits for them, and re-layouts, local(): lax.all_gather(spectra, 'lat', axis=4, tiled=True)  16.6 us
    all_gather x1, blocking collectives, local(): lax.all_gather(returned, 'lat', axis=0, tiled=True)  14.4 us
  transfers between devices with their start and end apart: 4, of which 3 were waited for; matrix products, arithmetic and copies ran while one was open for 56% of the time, Pallas kernels for 0%

commit v1 on v0

--- a/solution.py
+++ b/solution.py
@@ -6,6 +6,18 @@
 NLON = 3088
 lon_block = 512
 two_pi = 6.283185307179586
+
+
+def collect(array, axis, dim):
+    ways, here, turn = (lax.axis_size(axis), lax.axis_index(axis), array.shape[dim])
+    shape = [n * ways if d == dim else n for d, n in enumerate(array.shape)]
+    full = lax.dynamic_update_slice_in_dim(
+        jnp.zeros(shape, array.dtype), array, here * turn, axis=dim
+    )
+    for far in range(1, ways):
+        array = lax.ppermute(array, axis, [(d, (d + 1) % ways) for d in range(ways)])
+        full = lax.dynamic_update_slice_in_dim(full, array, (here - far) % ways * turn, axis=dim)
+    return full
 
 
 def block_count():
@@ -97,7 +109,7 @@
     fourier = jnp.einsum(
         "lsn,fvpsn->lvfps",
         band_part,
-        lax.all_gather(spectra, "lat", axis=4, tiled=True),
+        collect(spectra, "lat", 4),
         preferred_element_type=jnp.float32,
     ).astype(jnp.bfloat16)
     fourier = fourier.reshape(band_rows, 3, 2, slot_count)

time: 327 us -> 1220 us (3.73)
  local copies, waits for them, and re-layouts: 31.6 us -> 833 us
  starting transfers between devices: 10.4 us -> 108 us
  between operations: 16.2 us -> 2.74 us
    dynamic_update_slice x0 -> x8, local copies, waits for them, and re-layouts: none -> 806 us  [the longest x7 783 us: collect(): lax.dynamic_update_slice_in_dim(full, array, (here - far) % ways * turn,...]
    ppermute x0 -> x7, starting transfers between devices: none -> 97.2 us  [collect(): lax.ppermute(array, axis, [(d, (d + 1) % ways) for d in range(ways)])]
    ppermute x0 -> x7, waiting for transfers between devices: none -> 55.6 us  [collect(): lax.ppermute(array, axis, [(d, (d + 1) % ways) for d in range(ways)])]
    all_gather x1 -> x0, waiting for transfers between devices: 47 us -> none  [local(): lax.all_gather(spectra, 'lat', axis=4, tiled=True)]
    all_gather x1 -> x0, local copies, waits for them, and re-layouts: 16.6 us -> none  [local(): lax.all_gather(spectra, 'lat', axis=4, tiled=True)]
  transfers between devices with their start and end apart: 4 -> 10, of which waited for: 3 -> 7; matrix products, arithmetic and copies ran while one was open for 56% -> 72% of each run, Pallas kernels for 0% -> 0%
where the time goes in v1:
time: 1220 us
  local copies, waits for them, and re-layouts  833 us (68%)
  other arithmetic  167 us (14%)
  starting transfers between devices  108 us (9%)
  waiting for transfers between devices  60.9 us (5%)
  matrix products  29.6 us (2%)
  blocking collectives  14.5 us (1%)
    dynamic_update_slice x7, local copies, waits for them, and re-layouts, collect(): lax.dynamic_update_slice_in_dim(full, array, (here - far) % ways * turn,...  783 us
    another operation x8, other arithmetic  153 us
    ppermute x7, starting transfers between devices, collect(): lax.ppermute(array, axis, [(d, (d + 1) % ways) for d in range(ways)])  97.2 us
    ppermute x7, waiting for transfers between devices, collect(): lax.ppermute(array, axis, [(d, (d + 1) % ways) for d in range(ways)])  55.6 us
  transfers between devices with their start and end apart: 10, of which 7 were waited for; matrix products, arithmetic and copies ran while one was open for 72% of the time, Pallas kernels for 0%

profile of v1, /device:TPU:0, one launch (start us, length us, event | category | flops | bytes accessed | tf_op | source)
XLA Modules:
  0.0 1220.1 jit_solution(8548029750530250746)
XLA Ops:
  0.5 11.8 collective-permute-done
  12.3 11.1 collective-permute-done.1
  23.4 11.1 collective-permute-done.2
  34.5 11.1 collective-permute-done.3
  45.6 0.8 dynamic_slice.15
  46.4 10.4 collective-permute-done.4
  57.0 1.6 copy.74
  58.7 0.6 copy.82
  59.4 1.3 fusion.32
  60.7 2.3 copy.93
  63.1 3.4 broadcast_in_dim.52
  66.4 23.2 %dynamic_update_slice.27 = bf16[3,2,2,192,768]{4,0,2,1,3:T(4,128)(2,1)} dynamic-update-slice(bf16[3,2,2,192,768]{4,0,2,1,3:T(4,128)(2,1)} %broadcast_in_dim.52, bf16[3,2,2,192,96]{4,0,2,1,3:T(4,128)(2,1)S(1)} %copy.74, s32[]{:T(128)} %constant.134.clone.1, s32[]{:T(128)} %constant.134.clone.1, s32[]{:T(128)} %constant.134.clone.1, s32[]{:T(128)} %constant.134.clone.1, s32[]{:T(128)S(6)} %select_n.130) | dynamic-update-slice | bytes 884740 | tf_op jit(solution)/shard_map/dynamic_update_slice | solution.py:14
  89.6 0.6 select_reduce_fusion.2
  90.3 96.7 %collective-permute-start.6 = (bf16[3,2,2,192,96]{4,3,2,1,0:T(8,128)(2,1)}, bf16[3,2,2,192,96]{4,3,2,1,0:T(8,128)(2,1)}, u32[]{:S(2)}, u32[]{:S(2)}) collective-permute-start(bf16[3,2,2,192,96]{4,3,2,1,0:T(8,128)(2,1)} %collective-permute-done.5), channel_id=1, source_target_pairs={{0,4},{4,8},{8,12},{12,16},{16,20},{20,24},{24,28},{28,0},{1,5},{5... | collective-permute-start | bytes 1327112 | tf_op jit(solution)/shard_map/ppermute | solution.py:18
  186.9 0.6 broadcast_compare_fusion.1
  187.5 2.2 broadcast_select_fusion
  190.2 126.3 %dynamic_update_slice.28 = bf16[3,2,2,192,768]{4,0,2,1,3:T(4,128)(2,1)} dynamic-update-slice(bf16[3,2,2,192,768]{4,0,2,1,3:T(4,128)(2,1)} %dynamic_update_slice.27, bf16[3,2,2,192,96]{4,0,2,1,3:T(4,128)(2,1)S(1)} %copy.75, s32[]{:T(128)} %constant.134.clone.1, s32[]{:T(128)} %constant.134.clone.1, s32[]{:T(128)} %constant.134.clone.1, s32[]{:T(128)} %constant.134.clone.1, s32[]{:T(128)S(6)} %select_n.132) | dynamic-update-slice | bytes 884740 | tf_op jit(solution)/shard_map/dynamic_update_slice | solution.py:19
  317.0 126.7 %dynamic_update_slice.29 = bf16[3,2,2,192,768]{4,0,2,1,3:T(4,128)(2,1)} dynamic-update-slice(bf16[3,2,2,192,768]{4,0,2,1,3:T(4,128)(2,1)} %dynamic_update_slice.28, bf16[3,2,2,192,96]{4,0,2,1,3:T(4,128)(2,1)S(1)} %copy.76, s32[]{:T(128)} %constant.134.clone.1, s32[]{:T(128)} %constant.134.clone.1, s32[]{:T(128)} %constant.134.clone.1, s32[]{:T(128)} %constant.134.clone.1, s32[]{:T(128)S(6)} %select_n.134) | dynamic-update-slice | bytes 884740 | tf_op jit(solution)/shard_map/dynamic_update_slice | solution.py:19
  444.2 126.7 %dynamic_update_slice.30 = bf16[3,2,2,192,768]{4,0,2,1,3:T(4,128)(2,1)} dynamic-update-slice(bf16[3,2,2,192,768]{4,0,2,1,3:T(4,128)(2,1)} %dynamic_update_slice.29, bf16[3,2,2,192,96]{4,0,2,1,3:T(4,128)(2,1)S(1)} %copy.77, s32[]{:T(128)} %constant.134.clone.1, s32[]{:T(128)} %constant.134.clone.1, s32[]{:T(128)} %constant.134.clone.1, s32[]{:T(128)} %constant.134.clone.1, s32[]{:T(128)S(6)} %select_n.136) | dynamic-update-slice | bytes 884740 | tf_op jit(solution)/shard_map/dynamic_update_slice | solution.py:19
  571.4 23.2 %dynamic_update_slice.31 = bf16[3,2,2,192,768]{4,0,2,1,3:T(4,128)(2,1)} dynamic-update-slice(bf16[3,2,2,192,768]{4,0,2,1,3:T(4,128)(2,1)} %dynamic_update_slice.30, bf16[3,2,2,192,96]{4,0,2,1,3:T(4,128)(2,1)S(1)} %copy.78, s32[]{:T(128)} %constant.134.clone.1, s32[]{:T(128)} %constant.134.clone.1, s32[]{:T(128)} %constant.134.clone.1, s32[]{:T(128)} %constant.134.clone.1, s32[]{:T(128)S(6)} %select_n.138) | dynamic-update-slice | bytes 884740 | tf_op jit(solution)/shard_map/dynamic_update_slice | solution.py:19
  594.7 1.6 copy.79
  596.2 126.7 %dynamic_update_slice.32 = bf16[3,2,2,192,768]{4,0,2,1,3:T(4,128)(2,1)} dynamic-update-slice(bf16[3,2,2,192,768]{4,0,2,1,3:T(4,128)(2,1)} %dynamic_update_slice.31, bf16[3,2,2,192,96]{4,0,2,1,3:T(4,128)(2,1)S(1)} %copy.79, s32[]{:T(128)} %constant.134.clone.1, s32[]{:T(128)} %constant.134.clone.1, s32[]{:T(128)} %constant.134.clone.1, s32[]{:T(128)} %constant.134.clone.1, s32[]{:T(128)S(6)} %select_n.140) | dynamic-update-slice | bytes 884740 | tf_op jit(solution)/shard_map/dynamic_update_slice | solution.py:19
  722.9 1.6 copy.80
  724.5 126.7 %dynamic_update_slice.33 = bf16[3,2,2,192,768]{4,0,2,1,3:T(4,128)(2,1)} dynamic-update-slice(bf16[3,2,2,192,768]{4,0,2,1,3:T(4,128)(2,1)} %dynamic_update_slice.32, bf16[3,2,2,192,96]{4,0,2,1,3:T(4,128)(2,1)S(1)} %copy.80, s32[]{:T(128)} %constant.134.clone.1, s32[]{:T(128)} %constant.134.clone.1, s32[]{:T(128)} %constant.134.clone.1, s32[]{:T(128)} %constant.134.clone.1, s32[]{:T(128)S(6)} %select_n.142) | dynamic-update-slice | bytes 884740 | tf_op jit(solution)/shard_map/dynamic_update_slice | solution.py:19
  851.2 1.6 copy.81
  852.8 126.7 %dynamic_update_slice.34 = bf16[3,2,2,192,768]{4,0,2,1,3:T(4,128)(2,1)} dynamic-update-slice(bf16[3,2,2,192,768]{4,0,2,1,3:T(4,128)(2,1)} %dynamic_update_slice.33, bf16[3,2,2,192,96]{4,0,2,1,3:T(4,128)(2,1)S(1)} %copy.81, s32[]{:T(128)} %constant.134.clone.1, s32[]{:T(128)} %constant.134.clone.1, s32[]{:T(128)} %constant.134.clone.1, s32[]{:T(128)} %constant.134.clone.1, s32[]{:T(128)S(6)} %select_n.144) | dynamic-update-slice | bytes 884740 | tf_op jit(solution)/shard_map/dynamic_update_slice | solution.py:19
  979.5 23.1 %fusion.19 = bf16[2,2,3,2,192]{2,0,3,1,4:T(2,128)(2,1)S(1)} fusion(bf16[3,2,2,192,768]{4,0,2,1,3:T(4,128)(2,1)} %dynamic_update_slice.34, bf16[2,192,768,1,1]{2,0,4,3,1:T(2,128)(2,1)S(1)} %copy-done.7), kind=kOutput, calls=%fused_computation.33 | convolution fusion | flops 7082496 | bytes 4137984 | tf_op jit(solution)/shard_map/lsn,fvpsn->lvfps/dot_general | solution.py:109
  1002.7 1.1 copy.84
  1003.7 3.7 all-to-all-start
  1007.5 0.7 select_reduce_fusion
  1010.5 1.7 all-to-all-done
  1012.2 3.8 all-to-all-start.2
  1016.2 176.5 %while.20 = (s32[]{:T(128)}, f32[2,1536]{1,0:T(2,128)S(1)}, s32[7]{0:T(128)S(1)}, s32[]{:T(128)}, s32[768]{0:T(1024)S(1)}, /*index=5*/s32[]{:T(128)}, pred[]{:T(...) while((s32[]{:T(128)}, f32[2,1536]{1,0:T(2,128)S(1)}, ...), condition=%wide.region_3.4_spmd.clone, body=%wide.region_2.3_spmd.clone.sunk | while | flops 19283972 | bytes 4777144 | solution.py:83
  1016.2 0.7 dynamic_slice.18
  1017.5 21.8 %cosine_convert_fusion.2 = (bf16[512,768]{1,0:T(8,128)(2,1)S(1)}, bf16[512,768]{1,0:T(8,128)(2,1)S(1)}) fusion(f32[]{:T(128)} %get-tuple-element.295, pred[]{:T(512)} %get-tuple-element.294, s32[]{:T(128)} %get-tuple-element.293, s32[768]{0:T(1024)S(1)} %get-tuple-element.292, s32[512]{0:T(512)S(1)} %iota_add_fusion.2), kind=kLoop, calls=%fused_computation.7.clone.1 | loop fusion | flops 5111808 | bytes 1577993 | tf_op jit(solution)/shard_map/convert
  1039.8 0.7 fusion.38
  1040.5 0.6 broadcast_compare_fusion.3
  1041.4 0.7 dynamic_slice.18
  1042.7 21.8 %cosine_convert_fusion.2 = (bf16[512,768]{1,0:T(8,128)(2,1)S(1)}, bf16[512,768]{1,0:T(8,128)(2,1)S(1)}) fusion(f32[]{:T(128)} %get-tuple-element.295, pred[]{:T(512)} %get-tuple-element.294, s32[]{:T(128)} %get-tuple-element.293, s32[768]{0:T(1024)S(1)} %get-tuple-element.292, s32[512]{0:T(512)S(1)} %iota_add_fusion.2), kind=kLoop, calls=%fused_computation.7.clone.1 | loop fusion | flops 5111808 | bytes 1577993 | tf_op jit(solution)/shard_map/convert
  1065.0 0.7 fusion.38
  1065.7 0.6 broadcast_compare_fusion.3
  1066.6 0.7 dynamic_slice.18
  1067.9 21.8 %cosine_convert_fusion.2 = (bf16[512,768]{1,0:T(8,128)(2,1)S(1)}, bf16[512,768]{1,0:T(8,128)(2,1)S(1)}) fusion(f32[]{:T(128)} %get-tuple-element.295, pred[]{:T(512)} %get-tuple-element.294, s32[]{:T(128)} %get-tuple-element.293, s32[768]{0:T(1024)S(1)} %get-tuple-element.292, s32[512]{0:T(512)S(1)} %iota_add_fusion.2), kind=kLoop, calls=%fused_computation.7.clone.1 | loop fusion | flops 5111808 | bytes 1577993 | tf_op jit(solution)/shard_map/convert
  1090.2 0.7 fusion.38
  1091.8 0.7 dynamic_slice.18
  1093.1 21.8 %cosine_convert_fusion.2 = (bf16[512,768]{1,0:T(8,128)(2,1)S(1)}, bf16[512,768]{1,0:T(8,128)(2,1)S(1)}) fusion(f32[]{:T(128)} %get-tuple-element.295, pred[]{:T(512)} %get-tuple-element.294, s32[]{:T(128)} %get-tuple-element.293, s32[768]{0:T(1024)S(1)} %get-tuple-element.292, s32[512]{0:T(512)S(1)} %iota_add_fusion.2), kind=kLoop, calls=%fused_computation.7.clone.1 | loop fusion | flops 5111808 | bytes 1577993 | tf_op jit(solution)/shard_map/convert
  1115.4 0.7 fusion.38
  1117.1 0.7 dynamic_slice.18
  1118.4 21.8 %cosine_convert_fusion.2 = (bf16[512,768]{1,0:T(8,128)(2,1)S(1)}, bf16[512,768]{1,0:T(8,128)(2,1)S(1)}) fusion(f32[]{:T(128)} %get-tuple-element.295, pred[]{:T(512)} %get-tuple-element.294, s32[]{:T(128)} %get-tuple-element.293, s32[768]{0:T(1024)S(1)} %get-tuple-element.292, s32[512]{0:T(512)S(1)} %iota_add_fusion.2), kind=kLoop, calls=%fused_computation.7.clone.1 | loop fusion | flops 5111808 | bytes 1577993 | tf_op jit(solution)/shard_map/convert
  1140.7 0.7 fusion.38
  1142.3 0.7 dynamic_slice.18
  1143.6 21.8 %cosine_convert_fusion.2 = (bf16[512,768]{1,0:T(8,128)(2,1)S(1)}, bf16[512,768]{1,0:T(8,128)(2,1)S(1)}) fusion(f32[]{:T(128)} %get-tuple-element.295, pred[]{:T(512)} %get-tuple-element.294, s32[]{:T(128)} %get-tuple-element.293, s32[768]{0:T(1024)S(1)} %get-tuple-element.292, s32[512]{0:T(512)S(1)} %iota_add_fusion.2), kind=kLoop, calls=%fused_computation.7.clone.1 | loop fusion | flops 5111808 | bytes 1577993 | tf_op jit(solution)/shard_map/convert
  1165.9 0.7 fusion.38
  1167.5 0.7 dynamic_slice.18
  1168.8 21.8 %cosine_convert_fusion.2 = (bf16[512,768]{1,0:T(8,128)(2,1)S(1)}, bf16[512,768]{1,0:T(8,128)(2,1)S(1)}) fusion(f32[]{:T(128)} %get-tuple-element.295, pred[]{:T(512)} %get-tuple-element.294, s32[]{:T(128)} %get-tuple-element.293, s32[768]{0:T(1024)S(1)} %get-tuple-element.292, s32[512]{0:T(512)S(1)} %iota_add_fusion.2), kind=kLoop, calls=%fused_computation.7.clone.1 | loop fusion | flops 5111808 | bytes 1577993 | tf_op jit(solution)/shard_map/convert
  1191.1 0.7 fusion.38
  1193.2 1.1 reshape.136
  1194.3 3.2 all-to-all-start.1
  1197.5 1.0 copy.90
  1198.5 3.7 all-to-all-done.1
  1202.2 0.8 reshape.137
  1203.4 14.5 %all_gather.3 = bf16[16,2,2,2,192]{4,3,2,1,0:T(2,128)(2,1)S(1)} all-gather(bf16[2,2,2,2,192]{4,3,2,1,0:T(2,128)(2,1)S(1)} %bitcast.68), channel_id=1, replica_groups=mesh['lat'=8,'wave'=4] {'lat'}, dimensions={0}, use_global_device_ids=true | all-gather | bytes 55296 | tf_op jit(solution)/shard_map/all_gather | solution.py:134
  1218.3 0.7 convolution_bitcast_fusion.1
  1219.0 1.0 copy.92
  (77 shorter events, 12.8 us)
Async XLA Ops:
  0.0 58.7 %copy-start = (bf16[2,192,768]{2,1,0:T(8,128)(2,1)S(1)}, bf16[2,192,768]{2,1,0:T(8,128)(2,1)}, u32[]{:S(2)}) copy-start(bf16[2,192,768]{2,1,0:T(8,128)(2,1)} %param.9) | copy-start | bytes 1769476
  0.0 12.3 %collective-permute-start = (bf16[3,2,2,192,96]{4,3,2,1,0:T(8,128)(2,1)}, bf16[3,2,2,192,96]{4,3,2,1,0:T(8,128)(2,1)S(1)}, u32[]{:S(2)}, u32[]{:S(2)}) collective-permute-start(bf16[3,2,2,192,96]{4,3,2,1,0:T(8,128)(2,1)} %param.8), channel_id=1, source_target_pairs={{0,4},{4,8},{8,12},{12,16},{16,20},{20,24},{24,28},{28,0},{1,5},{5... | collective-permute-start | bytes 1327112 | tf_op jit(solution)/shard_map/ppermute | solution.py:18
  12.3 11.1 collective-permute-start.1
  23.4 33.6 %copy-start.1 = (bf16[3,2,2,192,96]{4,3,2,1,0:T(8,128)(2,1)}, bf16[3,2,2,192,96]{4,3,2,1,0:T(8,128)(2,1)S(1)}, u32[]{:S(2)}) copy-start(bf16[3,2,2,192,96]{4,3,2,1,0:T(8,128)(2,1)S(1)} %collective-permute-done.1) | copy-start | bytes 1327108
  23.4 11.1 collective-permute-start.2
  34.5 22.3 %copy-start.3 = (bf16[3,2,2,192,96]{4,3,2,1,0:T(8,128)(2,1)}, bf16[3,2,2,192,96]{4,3,2,1,0:T(8,128)(2,1)S(1)}, u32[]{:S(2)}) copy-start(bf16[3,2,2,192,96]{4,3,2,1,0:T(8,128)(2,1)S(1)} %collective-permute-done.2) | copy-start | bytes 1327108
  34.5 11.1 collective-permute-start.3
  45.6 13.1 %copy-start.5 = (bf16[3,2,2,192,96]{4,3,2,1,0:T(8,128)(2,1)}, bf16[3,2,2,192,96]{4,3,2,1,0:T(8,128)(2,1)S(1)}, u32[]{:S(2)}) copy-start(bf16[3,2,2,192,96]{4,3,2,1,0:T(8,128)(2,1)S(1)} %collective-permute-done.3) | copy-start | bytes 1327108
  45.6 11.2 collective-permute-start.4
  56.8 33.4 %collective-permute-start.5 = (bf16[3,2,2,192,96]{4,3,2,1,0:T(8,128)(2,1)}, bf16[3,2,2,192,96]{4,3,2,1,0:T(8,128)(2,1)}, u32[]{:S(2)}, u32[]{:S(2)}) collective-permute-start(bf16[3,2,2,192,96]{4,3,2,1,0:T(8,128)(2,1)} %collective-permute-done.4), channel_id=1, source_target_pairs={{0,4},{4,8},{8,12},{12,16},{16,20},{20,24},{24,28},{28,0},{1,5},{5... | collective-permute-start | bytes 1327112 | tf_op jit(solution)/shard_map/ppermute | solution.py:18
  66.4 23.2 %copy-start.11 = (s32[2]{0:T(128)S(1)}, s32[2]{0:T(128)}, u32[]{:S(2)}) copy-start(s32[2]{0:T(128)} %param.11) | copy-start | bytes 28
  66.4 120.5 %copy-start.8 = (s32[768]{0:T(1024)S(1)}, s32[768]{0:T(1024)}, u32[]{:S(2)}) copy-start(s32[768]{0:T(1024)} %param.10) | copy-start | bytes 9220
  90.3 760.9 %collective-permute-start.6 = (bf16[3,2,2,192,96]{4,3,2,1,0:T(8,128)(2,1)}, bf16[3,2,2,192,96]{4,3,2,1,0:T(8,128)(2,1)}, u32[]{:S(2)}, u32[]{:S(2)}) collective-permute-start(bf16[3,2,2,192,96]{4,3,2,1,0:T(8,128)(2,1)} %collective-permute-done.5), channel_id=1, source_target_pairs={{0,4},{4,8},{8,12},{12,16},{16,20},{20,24},{24,28},{28,0},{1,5},{5... | collective-permute-start | bytes 1327112 | tf_op jit(solution)/shard_map/ppermute | solution.py:18
  189.7 126.8 %copy-start.2 = (bf16[3,2,2,192,96]{4,3,2,1,0:T(8,128)(2,1)S(1)}, bf16[3,2,2,192,96]{4,3,2,1,0:T(8,128)(2,1)}, u32[]{:S(2)}) copy-start(bf16[3,2,2,192,96]{4,3,2,1,0:T(8,128)(2,1)} %copy-done.1) | copy-start | bytes 1327108
  316.5 127.2 %copy-start.4 = (bf16[3,2,2,192,96]{4,3,2,1,0:T(8,128)(2,1)S(1)}, bf16[3,2,2,192,96]{4,3,2,1,0:T(8,128)(2,1)}, u32[]{:S(2)}) copy-start(bf16[3,2,2,192,96]{4,3,2,1,0:T(8,128)(2,1)} %copy-done.3) | copy-start | bytes 1327108
  443.7 127.2 %copy-start.6 = (bf16[3,2,2,192,96]{4,3,2,1,0:T(8,128)(2,1)S(1)}, bf16[3,2,2,192,96]{4,3,2,1,0:T(8,128)(2,1)}, u32[]{:S(2)}) copy-start(bf16[3,2,2,192,96]{4,3,2,1,0:T(8,128)(2,1)} %copy-done.5) | copy-start | bytes 1327108
  851.2 128.3 %copy-start.7 = (bf16[2,192,768,1,1]{2,0,4,3,1:T(2,128)(2,1)S(1)}, bf16[2,192,768,1,1]{2,0,4,3,1:T(2,128)(2,1)}, u32[]{:S(2)}) copy-start(bf16[2,192,768,1,1]{2,0,4,3,1:T(2,128)(2,1)} %copy.93) | copy-start | bytes 1769476
  979.5 27.9 %copy-start.9 = (f32[2]{0:T(128)S(1)}, f32[2]{0:T(128)}, u32[]{:S(2)}) copy-start(f32[2]{0:T(128)} %param.13) | copy-start | bytes 28
  979.5 27.9 %copy-start.10 = (f32[2]{0:T(128)S(1)}, f32[2]{0:T(128)}, u32[]{:S(2)}) copy-start(f32[2]{0:T(128)} %param.12) | copy-start | bytes 28
  1003.7 8.4 all-to-all-start
  1012.2 182.1 %all-to-all-start.2 = ((bf16[2,192,768]{1,0,2:T(2,128)(2,1)}), bf16[2,192,768]{1,0,2:T(2,128)(2,1)S(1)}, u32[]{:S(2)}, u32[]{:S(2)}) async-start(bf16[2,192,768]{1,0,2:T(2,128)(2,1)} %broadcast_select_fusion), calls=%async_computation.2 | async-start | bytes 1572864 | tf_op jit(solution)/shard_map/all_to_all | solution.py:129
  1194.3 7.9 all-to-all-start.1
